TPU v7x, 512 devices: a whole 4x4x16 slice. The times are simulated.
512 devices in a mesh: sample: 4 (over y), row: 8 (over x, core), col: 16 (over z).
Axes of the slice: x: 4, y: 4, z: 16, core: 2. Of those that a mesh axis runs over, the one named last changes fastest.
Arguments:
- pair: bfloat16 [3584, 896, 128], P(('sample', 'row'), 'col'), parts along dimension 0, may hold values from -6 to 6
- pair_gain: float32 [128], replicated, may hold values from 0.1 to 1.9
- bias_weight: bfloat16 [128, 16], replicated, may hold values from -0.5 to 0.5
- single: bfloat16 [3584, 384], P(('sample', 'row', 'col')), parts along dimension 0, may hold values from -50 to 50
- w_query: bfloat16 [384, 384], replicated, may hold values from -0.30618622 to 0.30618622
- w_key: bfloat16 [384, 384], replicated, may hold values from -0.30618622 to 0.30618622
- w_value: bfloat16 [384, 384], replicated, may hold values from -0.3125 to 0.3125
- w_out: bfloat16 [384, 384], replicated, may hold values from -0.3125 to 0.3125
- key_mask: int32 [3584], P(('sample', 'col')), parts along dimension 0, may hold values from 0 to 1, as said below
- out_grad: bfloat16 [3584, 384], P(('sample', 'row', 'col')), parts along dimension 0, may hold values from -6 to 6
Outputs:
- pair_grad: bfloat16 [3584, 896, 128], P(('sample', 'row'), 'col'), parts along dimension 0
- single_grad: bfloat16 [3584, 384], P(('sample', 'row', 'col')), parts along dimension 0
- query_weight_grad: float32 [1536, 384], P(('sample', 'row', 'col')), parts along dimension 0
- key_weight_grad: float32 [1536, 384], P(('sample', 'row', 'col')), parts along dimension 0
- value_weight_grad: float32 [1536, 384], P(('sample', 'row', 'col')), parts along dimension 0
- out_weight_grad: float32 [1536, 384], P(('sample', 'row', 'col')), parts along dimension 0
- bias_weight_grad: float32 [512, 16], P('sample'), parts along dimension 0
- gain_grad: float32 [512], P('sample'), parts along dimension 0
There are 4 independent parts, one for each index of `sample`. A program takes and returns all parts, laid end to end along the dimension named above; an argument that names none is the same for every part. Nothing has to cross between parts.
Inputs may be any that keep to these rules, and one draw needn't show every extreme that they name: key_mask is 1 exactly on a prefix of the tokens whose length is a multiple of 4, at least half of 896 and at most 892, and 0 after it.
All inputs are finite; a program needn't handle non-finite values.
Results may differ from a plain program's by a relative error of at most 0.04.
Values may be sent and summed in bfloat16 or wider, within the bound.
No kernel may reach another device: no remote copies, remote signals or barrier semaphores. Data moves between devices by JAX's collectives and lax.ppermute only.
A program may use at most 64 MiB of HBM per device.

v0:
```python
import functools
import jax
import jax.numpy as jnp
from jax import lax
from jax.sharding import Mesh
from jax.sharding import PartitionSpec as P

HEADS = 16
HEAD = 24
ROW = ("row_0", "row_1")
ROW_COL = ("row_0", "row_1", "col")
SAMPLE_ROW = ("sample", "row_0", "row_1")
SAMPLE_ROW_COL = ("sample", "row_0", "row_1", "col")
norm_eps = 1e-05
masked_score = -1000000000.0
highest = lax.Precision.HIGHEST


def laid_out(pieces, dim):
    shape = list(pieces.shape[1:])
    shape[dim] *= pieces.shape[0]
    return jnp.moveaxis(pieces, 0, dim).reshape(shape)


def stacked_from(array, axes, sequence):
    pieces = array[None]
    for k in sequence:
        pieces = lax.all_gather(pieces, axes[k], axis=0, tiled=True)
    carried = [lax.axis_size(axes[k]) for k in reversed(sequence)]
    pieces = pieces.reshape(*carried, *array.shape)
    turned = sorted(range(len(sequence)), key=lambda place: sequence[len(sequence) - 1 - place])
    return pieces.transpose(*turned, *range(len(sequence), pieces.ndim)).reshape(-1, *array.shape)


def gather_axes(array, axes, sequence, dim):
    return laid_out(stacked_from(array, axes, sequence), dim)


def from_everyone(array, axis):
    devices = lax.axis_size(axis)
    return lax.all_to_all(
        jnp.broadcast_to(array[None], (devices, *array.shape)), axis, 0, 0, tiled=True
    )


def gather_directly(array, axis, dim):
    pieces = from_everyone(array, axis)
    return laid_out(pieces, dim)


def collected_together(array, axis):
    leaves = jax.tree.leaves(array)
    sequence = sorted(range(len(leaves)), key=lambda k: -leaves[k].size)
    width = (1, *leaves[sequence[0]].shape)[-1]
    lines = [
        jnp.pad(leaves[k].reshape(-1), (0, -leaves[k].size % width)).reshape(-1, width)
        for k in sequence
    ]
    both, at, found = (from_everyone(jnp.concatenate(lines), axis), 0, {})
    for k, line in zip(sequence, lines):
        slab = both[:, at : at + len(line)].reshape(len(both), -1)
        found[k] = slab[:, : leaves[k].size].reshape(-1, *leaves[k].shape)
        at += len(line)
    numbers = iter(range(len(leaves)))
    return jax.tree.map(lambda _: found[next(numbers)], array)


def joined_by_halves(pieces, combine):
    while len(jax.tree.leaves(pieces)[0]) > 1:
        pieces = jax.vmap(combine)(
            *(jax.tree.map(lambda part: part[side::2], pieces) for side in (0, 1))
        )
    return jax.tree.map(lambda part: part[0], pieces)


def joined_all(array, axis, combine):
    pieces = collected_together(array, axis)
    return joined_by_halves(pieces, combine)


def over_pieces(array, axis):
    pieces = lax.all_gather(array, axis)
    return pieces.sum(axis=0)


def over_axes(array, axes):
    return functools.reduce(lax.psum, axes, array)


def taken_together(array, axis):
    everything = from_everyone(array, axis)
    return jnp.sum(everything.astype(jnp.float32), axis=0)


def broadcast(array, axis, root):
    return lax.dynamic_index_in_dim(lax.all_gather(array, axis), root, 0, keepdims=False)


def split_up(array, dim, devices):
    before, after = (array.shape[:dim], array.shape[dim + 1 :])
    return jnp.moveaxis(array.reshape(*before, devices, -1, *after), dim, 0)


def sum_at_owner(array, axis, dim):
    devices = lax.axis_size(axis)
    pieces = lax.all_to_all(split_up(array, dim, devices), axis, 0, 0, tiled=True)
    return jnp.sum(pieces.astype(jnp.float32), axis=0)


def sent_together(arrays, axis, dim, along):
    widths = [a.shape[along] for a in arrays]
    both = jnp.concatenate(arrays, axis=along)
    filled = sum_at_owner(both, axis, dim)
    return tuple(jnp.split(filled, [sum(widths[:k]) for k in range(1, len(widths))], axis=along))


def combine_stats(first, second):
    joint_top = jnp.maximum(first[0], second[0])
    joint_total = first[1] * jnp.exp(first[0] - joint_top) + second[1] * jnp.exp(
        second[0] - joint_top
    )
    return (joint_top, joint_total)


def project(grads, weight):
    return jnp.dot(grads, weight.astype(jnp.float32).T, precision=highest)


def transposed_product(left, right):
    return jnp.einsum("te,td->ed", left.astype(jnp.float32), right, precision=highest)


def body(pair, pair_gain, bias_weight, single, w_query, w_key, w_value, w_out, key_mask, out_grad):
    f32 = jnp.float32
    bf16 = jnp.bfloat16
    row_count = pair.shape[0]
    col_count = pair.shape[1]
    own_count = single.shape[0]
    model_width = single.shape[1]
    rows_total = lax.axis_size(ROW)
    cols_total = lax.axis_size("col")
    row_index = lax.axis_index(ROW)
    col_index = lax.axis_index("col")
    score_scale = HEAD ** (-0.5)
    all_single = gather_axes(single, ROW_COL, (2, 0, 1), 0)
    single_rows = lax.dynamic_slice_in_dim(all_single, row_index * row_count, row_count, 0)
    single_cols = lax.dynamic_slice_in_dim(all_single, col_index * col_count, col_count, 0)
    grad_rows = gather_directly(out_grad, "col", 0)
    query_rows = jnp.dot(single_rows, w_query, preferred_element_type=f32).astype(bf16)
    key_cols = jnp.dot(single_cols, w_key, preferred_element_type=f32).astype(bf16)
    value_cols = jnp.dot(single_cols, w_value, preferred_element_type=f32).astype(bf16)
    pair_float = pair.astype(f32)
    centred = pair_float - jnp.mean(pair_float, axis=2, keepdims=True)
    inverse = lax.rsqrt(jnp.mean(centred * centred, axis=2, keepdims=True) + norm_eps)
    normed = centred * inverse
    pair_normed = (normed * pair_gain).astype(bf16)
    pair_bias = jnp.einsum("ijc,ch->hij", pair_normed, bias_weight, preferred_element_type=f32)
    query_heads = query_rows.reshape(row_count, HEADS, HEAD)
    key_heads = key_cols.reshape(col_count, HEADS, HEAD)
    value_heads = value_cols.reshape(col_count, HEADS, HEAD)
    scores = (
        jnp.einsum("ihd,jhd->hij", query_heads, key_heads, preferred_element_type=f32) * score_scale
        + pair_bias
    )
    scores = jnp.where(key_mask[None, None, :] > 0, scores, masked_score)
    local_top = jnp.max(scores, axis=2)
    local_exp = jnp.exp(scores - local_top[:, :, None])
    row_top, row_total = joined_all((local_top, jnp.sum(local_exp, axis=2)), "col", combine_stats)
    exp_scores = local_exp * jnp.exp(local_top - row_top)[:, :, None]
    probs = exp_scores / row_total[:, :, None]
    probs_low = probs.astype(bf16)
    attended_part = jnp.einsum(
        "hij,jhd->ihd", probs_low, value_heads, preferred_element_type=f32
    ).reshape(row_count, model_width)
    attended = over_pieces(attended_part, "col")
    attended_low = attended.astype(bf16)
    grad_att = jnp.dot(grad_rows, w_out.T, preferred_element_type=f32).astype(bf16)
    grad_heads = grad_att.reshape(row_count, HEADS, HEAD)
    grad_probs = jnp.einsum("ihd,jhd->hij", grad_heads, value_heads, preferred_element_type=f32)
    row_delta = jnp.einsum(
        "ihd,ihd->hi", grad_heads.astype(f32), attended.reshape(row_count, HEADS, HEAD)
    )
    grad_scores = probs * (grad_probs - row_delta[:, :, None])
    grad_low = grad_scores.astype(bf16)
    query_grad = (
        jnp.einsum("hij,jhd->ihd", grad_low, key_heads, preferred_element_type=f32) * score_scale
    ).reshape(row_count, model_width)
    key_grad = (
        jnp.einsum("hij,ihd->jhd", grad_low, query_heads, preferred_element_type=f32) * score_scale
    ).reshape(col_count, model_width)
    value_grad = jnp.einsum(
        "hij,ihd->jhd", probs_low, grad_heads, preferred_element_type=f32
    ).reshape(col_count, model_width)
    grad_normed = jnp.einsum("hij,ch->ijc", grad_low, bias_weight, preferred_element_type=f32)
    bias_grad_part = jnp.einsum("ijc,hij->ch", pair_normed, grad_low, preferred_element_type=f32)
    gain_grad_part = jnp.sum(grad_normed * normed, axis=(0, 1))
    bias_weight_grad, gain_grad = (
        over_axes(bias_grad_part, ROW_COL),
        over_axes(gain_grad_part, ROW_COL),
    )
    scaled = grad_normed * pair_gain
    pair_grad = (
        inverse
        * (
            scaled
            - jnp.mean(scaled, axis=2, keepdims=True)
            - normed * jnp.mean(scaled * normed, axis=2, keepdims=True)
        )
    ).astype(bf16)
    own_start = col_index * own_count
    query_sum = taken_together(query_grad.astype(jnp.bfloat16), "col").astype(jnp.float32)
    key_sum, value_sum = (
        taken_together(key_grad.astype(jnp.bfloat16), ROW).astype(jnp.float32),
        taken_together(value_grad.astype(jnp.bfloat16), ROW).astype(jnp.float32),
    )
    own_query = lax.dynamic_slice_in_dim(query_sum, own_start, own_count, 0)
    own_part = project(own_query, w_query)
    key_side = project(key_sum, w_key) + project(value_sum, w_value)
    spread = cols_total // rows_total
    token_start = (row_index * cols_total + col_index) * own_count
    own_root = token_start // col_count
    offset = token_start - own_root * col_count
    for branch in range(spread):
        root_col = row_index * spread + branch
        fetched = broadcast(key_side.astype(jnp.bfloat16), "col", root_col).astype(key_side.dtype)
        piece = lax.dynamic_slice_in_dim(fetched, offset, own_count, 0)
        own_part = own_part + jnp.where(own_root == root_col, piece, 0.0)
    single_grad = own_part.astype(bf16)
    rows_each = model_width // (rows_total * cols_total)
    picked = lax.dynamic_index_in_dim(
        single_rows.reshape(row_count, rows_total, cols_total, rows_each),
        col_index,
        2,
        keepdims=False,
    ).reshape(row_count, rows_total * rows_each)
    att_picked = lax.dynamic_index_in_dim(
        attended_low.reshape(row_count, rows_total, cols_total, rows_each),
        col_index,
        2,
        keepdims=False,
    ).reshape(row_count, rows_total * rows_each)
    query_terms = transposed_product(picked, query_sum)
    out_terms = jnp.einsum("te,td->ed", att_picked, grad_rows, preferred_element_type=f32)
    query_weight_grad, out_weight_grad = sent_together(
        (query_terms.astype(jnp.bfloat16), out_terms.astype(jnp.bfloat16)), ROW, 0, 1
    )
    col_slab = lax.dynamic_slice_in_dim(
        single_cols, row_index * cols_total * rows_each, cols_total * rows_each, 1
    )
    key_weight_grad, value_weight_grad = sent_together(
        (
            transposed_product(col_slab, key_sum).astype(jnp.bfloat16),
            transposed_product(col_slab, value_sum).astype(jnp.bfloat16),
        ),
        "col",
        0,
        1,
    )
    return (
        pair_grad,
        single_grad,
        query_weight_grad,
        key_weight_grad,
        value_weight_grad,
        out_weight_grad,
        bias_weight_grad,
        gain_grad,
    )


def solution(mesh):
    split = Mesh(
        mesh.devices.reshape(mesh.shape["sample"], 4, 2, mesh.shape["col"]),
        ("sample", "row_0", "row_1", "col"),
    )
    placed = (
        P(SAMPLE_ROW, "col", None),
        P(),
        P(),
        P(SAMPLE_ROW_COL, None),
        P(),
        P(),
        P(),
        P(),
        P(("sample", "col")),
        P(SAMPLE_ROW_COL, None),
    )
    return jax.shard_map(
        body,
        mesh=split,
        in_specs=placed,
        out_specs=(
            P(SAMPLE_ROW, "col", None),
            P(SAMPLE_ROW_COL, None),
            P(SAMPLE_ROW_COL, None),
            P(SAMPLE_ROW_COL, None),
            P(SAMPLE_ROW_COL, None),
            P(SAMPLE_ROW_COL, None),
            P("sample", None),
            P("sample"),
        ),
        check_vma=False,
    )
```

profile of v0, /device:TPU:1, one launch (start us, length us, event | category | flops | bytes accessed | tf_op | source)
XLA Modules:
  0.0 361.2 jit_solution(5775855662982069744)
XLA Ops:
  7.9 2.3 convert_reduce_fusion
  10.3 3.0 fusion.12
  13.4 29.8 %all-gather.2 = bf16[16,7,384]{2,1,0:T(8,128)(2,1)S(1)} all-gather(bf16[1,7,384]{2,1,0:T(8,128)(2,1)S(1)} %bitcast.105), channel_id=2, replica_groups=mesh['sample'=4,'row_0'=4,'row_1'=2,'col'=16] {'col'}, dimensions={0}, use_global_device_ids=true | all-gather | bytes 91392 | tf_op jit(solution)/shard_map/all_gather | solution.py:28
  43.2 9.9 %all_gather.21 = bf16[64,7,384]{2,0,1:T(8,128)(2,1)S(1)} all-gather(bf16[16,7,384]{2,0,1:T(8,128)(2,1)S(1)} %copy.76), channel_id=1, replica_groups=mesh['sample'=4,'row_0'=4,'row_1'=2,'col'=16] {'row_0'}, dimensions={0}, use_global_device_ids=true | all-gather | bytes 430080 | tf_op jit(solution)/shard_map/all_gather | solution.py:28
  53.1 12.5 %all_gather.22 = bf16[128,7,384]{2,0,1:T(8,128)(2,1)S(1)} all-gather(bf16[64,7,384]{2,0,1:T(8,128)(2,1)S(1)} %all_gather.21), channel_id=1, replica_groups=mesh['sample'=4,'row_0'=4,'row_1'=2,'col'=16] {'row_1'}, dimensions={0}, use_global_device_ids=true | all-gather | bytes 1032192 | tf_op jit(solution)/shard_map/all_gather | solution.py:28
  69.6 3.3 fusion.23
  72.9 1.5 copy.80
  75.7 6.4 %all-to-all-start = ((f32[16,32,112]{2,1,0:T(8,128)}), f32[16,32,112]{2,1,0:T(8,128)S(1)}, u32[]{:S(2)}, u32[]{:S(2)}) async-start(f32[16,32,112]{2,1,0:T(8,128)} %broadcast_in_dim.31), calls=%async_computation | async-start | bytes 524288 | tf_op jit(solution)/shard_map/all_to_all | solution.py:41
  83.3 12.8 %all-to-all-done = f32[16,32,112]{2,1,0:T(8,128)S(1)} async-done(((f32[16,32,112]{2,1,0:T(8,128)}), f32[16,32,112]{2,1,0:T(8,128)S(1)}, u32[]{:S(2)}, u32[]{:S(2)}) %all-to-all-start) | async-done | bytes 229408 | tf_op jit(solution)/shard_map/all_to_all | solution.py:41
  98.0 10.2 %all-to-all-start.1 = ((bf16[16,7,384]{2,1,0:T(8,128)(2,1)}), bf16[16,7,384]{2,1,0:T(8,128)(2,1)S(1)}, u32[]{:S(2)}, u32[]{:S(2)}) async-start(bf16[16,7,384]{2,1,0:T(8,128)(2,1)} %broadcast_in_dim.32), calls=%async_computation.1 | async-start | bytes 196608 | tf_op jit(solution)/shard_map/all_to_all | solution.py:41
  108.2 12.0 %all-to-all-done.1 = bf16[16,7,384]{2,1,0:T(8,128)(2,1)S(1)} async-done(((bf16[16,7,384]{2,1,0:T(8,128)(2,1)}), bf16[16,7,384]{2,1,0:T(8,128)(2,1)S(1)}, u32[]{:S(2)}, u32[]{:S(2)}) %all-to-all-start.1) | async-done | bytes 86048 | tf_op jit(solution)/shard_map/all_to_all | solution.py:41
  120.3 1.2 convolution_convert_fusion.1
  122.8 6.4 %all-to-all-start.4 = ((bf16[8,56,384]{2,1,0:T(8,128)(2,1)}), bf16[8,56,384]{2,1,0:T(8,128)(2,1)S(1)}, u32[]{:S(2)}, u32[]{:S(2)}) async-start(bf16[8,56,384]{2,1,0:T(8,128)(2,1)} %broadcast_in_dim.35), calls=%async_computation.4 | async-start | bytes 688128 | tf_op jit(solution)/shard_map/all_to_all | solution.py:41
  129.3 33.4 %all-gather.5.cloned.1.call-done = f32[16,112,384]{2,1,0:T(8,128)} async-done(((f32[1,112,384]{2,1,0:T(8,128)}), f32[16,112,384]{2,1,0:T(8,128)}) %all-gather.5.cloned.1.call-update) | async-done | bytes 2752528 | tf_op jit(solution)/shard_map/all_gather | solution.py:82
  162.7 1.9 reduce_sum.111
  167.1 13.5 %all-to-all-start.3 = ((bf16[8,56,384]{2,1,0:T(8,128)(2,1)}), bf16[8,56,384]{2,1,0:T(8,128)(2,1)S(1)}, u32[]{:S(2)}, u32[]{:S(2)}) async-start(bf16[8,56,384]{2,1,0:T(8,128)(2,1)} %broadcast_in_dim.34), calls=%async_computation.3 | async-start | bytes 688128 | tf_op jit(solution)/shard_map/all_to_all | solution.py:41
  181.8 6.1 %all-to-all-done.3 = bf16[8,56,384]{2,1,0:T(8,128)(2,1)S(1)} async-done(((bf16[8,56,384]{2,1,0:T(8,128)(2,1)}), bf16[8,56,384]{2,1,0:T(8,128)(2,1)S(1)}, u32[]{:S(2)}, u32[]{:S(2)}) %all-to-all-start.3) | async-done | bytes 344096 | tf_op jit(solution)/shard_map/all_to_all | solution.py:41
  189.7 7.4 %all-to-all-start.6 = ((bf16[16,3,768]{2,1,0:T(4,128)(2,1)}), bf16[16,3,768]{2,1,0:T(4,128)(2,1)S(1)}, u32[]{:S(2)}, u32[]{:S(2)}) async-start(bf16[16,3,768]{2,1,0:T(4,128)(2,1)} %reshape.139), calls=%async_computation.6 | async-start | bytes 196608 | tf_op jit(solution)/shard_map/all_to_all | solution.py:106
  198.3 10.6 %all-to-all-done.6 = bf16[16,3,768]{2,1,0:T(4,128)(2,1)S(1)} async-done(((bf16[16,3,768]{2,1,0:T(4,128)(2,1)}), bf16[16,3,768]{2,1,0:T(4,128)(2,1)S(1)}, u32[]{:S(2)}, u32[]{:S(2)}) %all-to-all-start.6) | async-done | bytes 73760 | tf_op jit(solution)/shard_map/all_to_all | solution.py:106
  210.2 4.6 %all-to-all-start.2 = ((bf16[16,112,384]{2,1,0:T(8,128)(2,1)}), bf16[16,112,384]{2,1,0:T(8,128)(2,1)S(1)}, u32[]{:S(2)}, u32[]{:S(2)}) async-start(bf16[16,112,384]{2,1,0:T(8,128)(2,1)} %broadcast_in_dim.33), calls=%async_computation.2 | async-start | bytes 2752512 | tf_op jit(solution)/shard_map/all_to_all | solution.py:41
  214.8 1.6 copy.89
  216.4 1.6 reshape.135
  219.4 1.6 convert_element_type.148
  225.1 3.8 %convolution_bitcast_fusion = f32[128,16]{0,1:T(8,128)S(1)} fusion(bf16[16,112,56]{2,0,1:T(8,128)(2,1)} %copy.85, bf16[112,56,128]{2,1,0:T(8,128)(2,1)S(1)} %copy-done.1, f32[128]{0:T(128)S(1)} %copy-done.28, f32[112,56]{1,0:T(8,128)} %copy-done.22, f32[112,56]{1,0:T(8,128)} %copy-done.17), kind=kOutput, calls=%fused_computation.41 | convolution fusion | flops 29704192 | bytes 1865216 | tf_op jit(solution)/shard_map/ijc,hij->ch/dot_general | solution.py:195
  229.0 6.4 %fusion.11 = (f32[128]{0:T(128)S(1)}, f32[112,56]{1,0:T(8,128)S(1)}, f32[112,56]{1,0:T(8,128)}, f32[112,56,128]{2,1,0:T(8,128)}) fusion(bf16[112,56,128]{2,1,0:T(8,128)(2,1)S(1)} %copy-done.1, f32[112,56]{1,0:T(8,128)S(1)} %copy-done.23, f32[112,56]{1,0:T(8,128)S(1)} %copy-done.18, f32[128]{0:T(128)} %param.11, bf16[16,112,56]{2,0,1:T(8,128)(2,1)S(1)} %copy-done.19, ...), kind=kOutput, calls=%fused_computation.13 | convolution fusion | flops 32902784 | bytes 5123072 | tf_op jit(solution)/shard_map/hij,ch->ijc/dot_general | solution.py:194
  235.4 8.1 %all-reduce.1 = (f32[128,16]{0,1:T(8,128)S(1)}, f32[128]{0:T(128)}) all-reduce(f32[128,16]{0,1:T(8,128)S(1)} %convolution_bitcast_fusion, f32[128]{0:T(128)S(1)} %get-tuple-element.8), channel_id=1, replica_groups=mesh['sample'=4,'row_0'=4,'row_1'=2,'col'=16] {'row_0'}, use_global_device_ids=true, to_apply=%region_12.13 | all-reduce | flops 2176 | bytes 17408 | tf_op jit(solution)/shard_map/psum | solution.py:87
  243.6 5.9 %all-reduce.2 = (f32[128,16]{0,1:T(8,128)S(1)}, f32[128]{0:T(128)S(1)}) all-reduce(f32[128,16]{0,1:T(8,128)S(1)} %get-tuple-element.13, f32[128]{0:T(128)} %get-tuple-element.14), channel_id=1, replica_groups=mesh['sample'=4,'row_0'=4,'row_1'=2,'col'=16] {'row_1'}, use_global_device_ids=true, to_apply=%region_13.14 | all-reduce | flops 2176 | bytes 17408 | tf_op jit(solution)/shard_map/psum | solution.py:87
  249.4 46.0 %all-reduce = (f32[128,16]{0,1:T(8,128)}, f32[128]{0:T(128)}) all-reduce(f32[128,16]{0,1:T(8,128)S(1)} %get-tuple-element.15, f32[128]{0:T(128)S(1)} %get-tuple-element.16), channel_id=1, replica_groups=mesh['sample'=4,'row_0'=4,'row_1'=2,'col'=16] {'col'}, use_global_device_ids=true, to_apply=%region_14.15 | all-reduce | flops 2176 | bytes 17408 | tf_op jit(solution)/shard_map/psum | solution.py:87
  297.2 7.7 %fusion.10 = bf16[112,56,128]{2,1,0:T(8,128)(2,1)} fusion(bf16[112,56,128]{2,1,0:T(8,128)(2,1)S(1)} %copy-done.1, f32[112,56,128]{2,1,0:T(8,128)} %get-tuple-element.31, f32[112,56]{1,0:T(8,128)S(1)} %get-tuple-element.32, f32[112,56]{1,0:T(8,128)S(1)} %get-tuple-element.33, f32[128]{0:T(128)} %param.11, f32[112,56]{1,0:T(8,128)S(1)} %copy-done.23, ...), kind=kLoop, calls=%fused_computation.12 | loop fusion | flops 7225344 | bytes 6523392 | tf_op jit(solution)/shard_map/convert_element_type | solution.py:209
  305.8 24.5 %all-gather.1 = bf16[896,384]{1,0:T(8,128)(2,1)S(1)} all-gather(bf16[56,384]{1,0:T(8,128)(2,1)S(1)} %fusion.19), channel_id=3, replica_groups=mesh['sample'=4,'row_0'=4,'row_1'=2,'col'=16] {'col'}, dimensions={0}, use_global_device_ids=true | all-gather | bytes 731136 | tf_op jit(solution)/shard_map/all_gather | solution.py:96
  332.0 16.9 %all-to-all-start.5 = ((bf16[8,3,768]{2,1,0:T(4,128)(2,1)}), bf16[8,3,768]{2,1,0:T(4,128)(2,1)S(1)}, u32[]{:S(2)}, u32[]{:S(2)}) async-start(bf16[8,3,768]{2,1,0:T(4,128)(2,1)} %reshape.138), calls=%async_computation.5 | async-start | bytes 98304 | tf_op jit(solution)/shard_map/all_to_all | solution.py:106
  349.9 3.8 %all-to-all-done.5 = bf16[8,3,768]{2,1,0:T(4,128)(2,1)S(1)} async-done(((bf16[8,3,768]{2,1,0:T(4,128)(2,1)}), bf16[8,3,768]{2,1,0:T(4,128)(2,1)S(1)}, u32[]{:S(2)}, u32[]{:S(2)}) %all-to-all-start.5) | async-done | bytes 36896 | tf_op jit(solution)/shard_map/all_to_all | solution.py:106
  (130 shorter events, 29.3 us)
Async XLA Ops:
  7.2 62.0 %copy-start = (bf16[384,384]{1,0:T(8,128)(2,1)S(1)}, bf16[384,384]{1,0:T(8,128)(2,1)}, u32[]{:S(2)}) copy-start(bf16[384,384]{1,0:T(8,128)(2,1)} %param.14) | copy-start | bytes 884740
  10.2 59.3 %copy-start.17 = (f32[112,56]{1,0:T(8,128)}, f32[112,56]{1,0:T(8,128)S(1)}, u32[]{:S(2)}) copy-start(f32[112,56]{1,0:T(8,128)S(1)} %broadcast_multiply_fusion.2) | copy-start | bytes 75268
  10.3 56.9 %copy-start.3 = (bf16[384,384]{1,0:T(8,128)(2,1)S(1)}, bf16[384,384]{1,0:T(8,128)(2,1)}, u32[]{:S(2)}) copy-start(bf16[384,384]{1,0:T(8,128)(2,1)} %param.15) | copy-start | bytes 884740
  13.3 56.3 %copy-start.1 = (bf16[112,56,128]{2,1,0:T(8,128)(2,1)S(1)}, bf16[112,56,128]{2,1,0:T(8,128)(2,1)}, u32[]{:S(2)}) copy-start(bf16[112,56,128]{2,1,0:T(8,128)(2,1)} %param.10) | copy-start | bytes 4816900
  13.3 56.2 %copy-start.28 = (f32[128]{0:T(128)S(1)}, f32[128]{0:T(128)}, u32[]{:S(2)}) copy-start(f32[128]{0:T(128)} %param.11) | copy-start | bytes 1540
  13.3 56.2 %copy-start.29 = (bf16[128,16]{0,1:T(8,128)(2,1)S(1)}, bf16[128,16]{0,1:T(8,128)(2,1)}, u32[]{:S(2)}) copy-start(bf16[128,16]{0,1:T(8,128)(2,1)} %param.12) | copy-start | bytes 12292
  13.4 59.5 %copy-start.22 = (f32[112,56]{1,0:T(8,128)}, f32[112,56]{1,0:T(8,128)S(1)}, u32[]{:S(2)}) copy-start(f32[112,56]{1,0:T(8,128)S(1)} %add_rsqrt_fusion) | copy-start | bytes 75268
  68.2 6.6 %copy-start.7 = (bf16[56,384]{0,1:T(8,128)(2,1)}, bf16[56,384]{0,1:T(8,128)(2,1)S(1)}, u32[]{:S(2)}) copy-start(bf16[56,384]{0,1:T(8,128)(2,1)S(1)} %copy.79) | copy-start | bytes 129028
  69.6 12.6 %copy-start.5 = (bf16[384,384]{1,0:T(8,128)(2,1)S(1)}, bf16[384,384]{1,0:T(8,128)(2,1)}, u32[]{:S(2)}) copy-start(bf16[384,384]{1,0:T(8,128)(2,1)} %param.16) | copy-start | bytes 884740
  74.5 22.9 %copy-start.27 = (bf16[7,384]{1,0:T(8,128)(2,1)S(1)}, bf16[7,384]{1,0:T(8,128)(2,1)}, u32[]{:S(2)}) copy-start(bf16[7,384]{1,0:T(8,128)(2,1)} %param.19) | copy-start | bytes 16132
  75.7 20.5 %all-to-all-start = ((f32[16,32,112]{2,1,0:T(8,128)}), f32[16,32,112]{2,1,0:T(8,128)S(1)}, u32[]{:S(2)}, u32[]{:S(2)}) async-start(f32[16,32,112]{2,1,0:T(8,128)} %broadcast_in_dim.31), calls=%async_computation | async-start | bytes 524288 | tf_op jit(solution)/shard_map/all_to_all | solution.py:41
  82.1 80.6 %all-gather.5.cloned.1.call-start = ((), (), s32[]{:S(2)}) async-start(), calls=%async_computation.7 | async-start | bytes 2924544 | tf_op jit(solution)/shard_map/all_gather | solution.py:82
  83.3 38.7 %copy-start.24 = (bf16[56,384]{0,1:T(8,128)(2,1)}, bf16[56,384]{0,1:T(8,128)(2,1)S(1)}, u32[]{:S(2)}) copy-start(bf16[56,384]{0,1:T(8,128)(2,1)S(1)} %copy.82) | copy-start | bytes 129028
  98.0 22.2 %all-to-all-start.1 = ((bf16[16,7,384]{2,1,0:T(8,128)(2,1)}), bf16[16,7,384]{2,1,0:T(8,128)(2,1)S(1)}, u32[]{:S(2)}, u32[]{:S(2)}) async-start(bf16[16,7,384]{2,1,0:T(8,128)(2,1)} %broadcast_in_dim.32), calls=%async_computation.1 | async-start | bytes 196608 | tf_op jit(solution)/shard_map/all_to_all | solution.py:41
  120.3 9.0 %copy-start.11 = (bf16[112,384]{1,0:T(8,128)(2,1)}, bf16[112,384]{1,0:T(8,128)(2,1)S(1)}, u32[]{:S(2)}) copy-start(bf16[112,384]{1,0:T(8,128)(2,1)S(1)} %reshape.131) | copy-start | bytes 258052
  122.8 43.2 %copy-start.9 = (bf16[112,384]{0,1:T(8,128)(2,1)S(1)}, bf16[112,384]{0,1:T(8,128)(2,1)}, u32[]{:S(2)}) copy-start(bf16[112,384]{0,1:T(8,128)(2,1)} %copy-done.8) | copy-start | bytes 258052
  122.8 43.5 %all-to-all-start.4 = ((bf16[8,56,384]{2,1,0:T(8,128)(2,1)}), bf16[8,56,384]{2,1,0:T(8,128)(2,1)S(1)}, u32[]{:S(2)}, u32[]{:S(2)}) async-start(bf16[8,56,384]{2,1,0:T(8,128)(2,1)} %broadcast_in_dim.35), calls=%async_computation.4 | async-start | bytes 688128 | tf_op jit(solution)/shard_map/all_to_all | solution.py:41
  164.6 33.6 %copy-start.2 = (f32[112,384]{1,0:T(8,128)}, f32[112,384]{1,0:T(8,128)S(1)}, u32[]{:S(2)}) copy-start(f32[112,384]{1,0:T(8,128)S(1)} %reduce_sum.111) | copy-start | bytes 516100
  167.1 20.7 %all-to-all-start.3 = ((bf16[8,56,384]{2,1,0:T(8,128)(2,1)}), bf16[8,56,384]{2,1,0:T(8,128)(2,1)S(1)}, u32[]{:S(2)}, u32[]{:S(2)}) async-start(bf16[8,56,384]{2,1,0:T(8,128)(2,1)} %broadcast_in_dim.34), calls=%async_computation.3 | async-start | bytes 688128 | tf_op jit(solution)/shard_map/all_to_all | solution.py:41
  180.7 29.5 %copy-start.15 = (f32[56,384]{1,0:T(8,128)}, f32[56,384]{1,0:T(8,128)S(1)}, u32[]{:S(2)}) copy-start(f32[56,384]{1,0:T(8,128)S(1)} %convert_reduce_fusion.2) | copy-start | bytes 258052
  187.9 22.3 %copy-start.13 = (f32[56,384]{1,0:T(8,128)}, f32[56,384]{1,0:T(8,128)S(1)}, u32[]{:S(2)}) copy-start(f32[56,384]{1,0:T(8,128)S(1)} %convert_reduce_fusion.3) | copy-start | bytes 258052
  189.7 19.3 %all-to-all-start.6 = ((bf16[16,3,768]{2,1,0:T(4,128)(2,1)}), bf16[16,3,768]{2,1,0:T(4,128)(2,1)S(1)}, u32[]{:S(2)}, u32[]{:S(2)}) async-start(bf16[16,3,768]{2,1,0:T(4,128)(2,1)} %reshape.139), calls=%async_computation.6 | async-start | bytes 196608 | tf_op jit(solution)/shard_map/all_to_all | solution.py:106
  210.2 120.8 %all-to-all-start.2 = ((bf16[16,112,384]{2,1,0:T(8,128)(2,1)}), bf16[16,112,384]{2,1,0:T(8,128)(2,1)S(1)}, u32[]{:S(2)}, u32[]{:S(2)}) async-start(bf16[16,112,384]{2,1,0:T(8,128)(2,1)} %broadcast_in_dim.33), calls=%async_computation.2 | async-start | bytes 2752512 | tf_op jit(solution)/shard_map/all_to_all | solution.py:41
  222.1 6.9 %copy-start.18 = (f32[112,56]{1,0:T(8,128)S(1)}, f32[112,56]{1,0:T(8,128)}, u32[]{:S(2)}) copy-start(f32[112,56]{1,0:T(8,128)} %copy-done.17) | copy-start | bytes 75268
  229.0 66.5 %copy-start.12 = (bf16[112,384]{1,0:T(8,128)(2,1)S(1)}, bf16[112,384]{1,0:T(8,128)(2,1)}, u32[]{:S(2)}) copy-start(bf16[112,384]{1,0:T(8,128)(2,1)} %copy-done.11) | copy-start | bytes 258052
  297.1 7.7 %copy-start.4 = (bf16[384,384]{1,0:T(8,128)(2,1)S(1)}, bf16[384,384]{1,0:T(8,128)(2,1)}, u32[]{:S(2)}) copy-start(bf16[384,384]{1,0:T(8,128)(2,1)} %param.15) | copy-start | bytes 884740
  297.1 7.7 %copy-start.14 = (f32[56,384]{1,0:T(8,128)S(1)}, f32[56,384]{1,0:T(8,128)}, u32[]{:S(2)}) copy-start(f32[56,384]{1,0:T(8,128)} %copy-done.13) | copy-start | bytes 258052
  297.2 8.1 %copy-start.6 = (bf16[384,384]{1,0:T(8,128)(2,1)S(1)}, bf16[384,384]{1,0:T(8,128)(2,1)}, u32[]{:S(2)}) copy-start(bf16[384,384]{1,0:T(8,128)(2,1)} %param.16) | copy-start | bytes 884740
  297.2 8.1 %copy-start.16 = (f32[56,384]{1,0:T(8,128)S(1)}, f32[56,384]{1,0:T(8,128)}, u32[]{:S(2)}) copy-start(f32[56,384]{1,0:T(8,128)} %copy-done.15) | copy-start | bytes 258052
  297.2 33.1 %copy-start.21 = (bf16[16,3,768]{2,1,0:T(4,128)(2,1)S(1)}, bf16[16,3,768]{2,1,0:T(4,128)(2,1)}, u32[]{:S(2)}) copy-start(bf16[16,3,768]{2,1,0:T(4,128)(2,1)} %copy-done.20) | copy-start | bytes 221188
  304.9 26.3 %copy-start.25 = (bf16[112,24]{0,1:T(8,128)(2,1)S(1)}, bf16[112,24]{0,1:T(8,128)(2,1)}, u32[]{:S(2)}) copy-start(bf16[112,24]{0,1:T(8,128)(2,1)} %reshape.136) | copy-start | bytes 16132
  332.0 21.7 %all-to-all-start.5 = ((bf16[8,3,768]{2,1,0:T(4,128)(2,1)}), bf16[8,3,768]{2,1,0:T(4,128)(2,1)S(1)}, u32[]{:S(2)}, u32[]{:S(2)}) async-start(bf16[8,3,768]{2,1,0:T(4,128)(2,1)} %reshape.138), calls=%async_computation.5 | async-start | bytes 98304 | tf_op jit(solution)/shard_map/all_to_all | solution.py:106
  (6 other events, 27.0 us)
Sparse Core Ops, SparseCore 0:
  97.5 65.1 all-gather.4
where the time goes:
time: 363 us; the launch traced here: 361 us
  blocking collectives  137 us (38%)
  waiting for transfers between devices  78.8 us (22%)
  starting transfers between devices  65.5 us (18%)
  matrix products  25.3 us (7%)
  local copies, waits for them, and re-layouts  21.3 us (6%)
  other arithmetic  18.7 us (5%)
  between operations  14.8 us (4%)
    psum x3, blocking collectives, over_axes(): return functools.reduce(lax.psum, axes, array)  60 us
    all_gather x3, blocking collectives, stacked_from(): pieces = lax.all_gather(pieces, axes[k], axis=0, tiled=True)  52.2 us
    all_to_all x5, starting transfers between devices, from_everyone(): lax.all_to_all(jnp.broadcast_to(array[None], (devices, *array.shape)), ax...  41.1 us
    all_gather x1, waiting for transfers between devices, over_pieces(): pieces = lax.all_gather(array, axis)  33.4 us
    all_to_all x5, waiting for transfers between devices, from_everyone(): lax.all_to_all(jnp.broadcast_to(array[None], (devices, *array.shape)), ax...  31 us
    all_gather x1, blocking collectives, broadcast(): lax.all_gather(array, axis)  24.5 us
    all_to_all x2, starting transfers between devices, sum_at_owner(): lax.all_to_all(split_up(array, dim, devices), axis, 0, 0, tiled=True)  24.3 us
    all_to_all x2, waiting for transfers between devices, sum_at_owner(): lax.all_to_all(split_up(array, dim, devices), axis, 0, 0, tiled=True)  14.4 us
  transfers between devices with their start and end apart: 8, of which 6 were waited for; matrix products, arithmetic and copies ran while one was open for 12% of the time, Pallas kernels for 0%

commit v1 on v0

--- a/solution.py
+++ b/solution.py
@@ -25,7 +25,9 @@
 def stacked_from(array, axes, sequence):
     pieces = array[None]
     for k in sequence:
-        pieces = lax.all_gather(pieces, axes[k], axis=0, tiled=True)
+        pieces = jnp.concatenate(
+            lax.all_to_all(jnp.stack([pieces] * lax.axis_size(axes[k])), axes[k], 0, 0), axis=0
+        )
     carried = [lax.axis_size(axes[k]) for k in reversed(sequence)]
     pieces = pieces.reshape(*carried, *array.shape)
     turned = sorted(range(len(sequence)), key=lambda place: sequence[len(sequence) - 1 - place])

time: 363 us -> 344 us (0.948)
  blocking collectives: 137 us -> 92.7 us
  starting transfers between devices: 65.5 us -> 81.2 us
  waiting for transfers between devices: 78.8 us -> 85.6 us
    all_gather x3 -> x0, blocking collectives: 52.2 us -> none  [stacked_from(): pieces = lax.all_gather(pieces, axes[k], axis=0, tiled=True)]
    all_to_all x0 -> x2, starting transfers between devices: none -> 19.7 us  [stacked_from(): lax.all_to_all(jnp.stack([pieces] * lax.axis_size(axes[k])), axes[k], 0, 0)]
    all_to_all x0 -> x1, blocking collectives: none -> 8.08 us  [stacked_from(): lax.all_to_all(jnp.stack([pieces] * lax.axis_size(axes[k])), axes[k], 0, 0)]
    all_to_all x0 -> x2, waiting for transfers between devices: none -> 7.53 us  [stacked_from(): lax.all_to_all(jnp.stack([pieces] * lax.axis_size(axes[k])), axes[k], 0, 0)]
    all_to_all x5, starting transfers between devices: 41.1 us -> 37.2 us  [from_everyone(): lax.all_to_all(jnp.broadcast_to(array[None], (devices, *array.shape)), ax...]
  transfers between devices with their start and end apart: 8 -> 10, of which waited for: 6 -> 8; matrix products, arithmetic and copies ran while one was open for 12% -> 15% of each run, Pallas kernels for 0% -> 0%
where the time goes in v1:
time: 344 us; the launch traced here: 342 us
  blocking collectives  92.7 us (27%)
  waiting for transfers between devices  85.6 us (25%)
  starting transfers between devices  81.2 us (24%)
  matrix products  25.4 us (7%)
  local copies, waits for them, and re-layouts  24.8 us (7%)
  other arithmetic  18 us (5%)
  between operations  14.7 us (4%)
    psum x3, blocking collectives, over_axes(): return functools.reduce(lax.psum, axes, array)  60.1 us
    all_to_all x5, starting transfers between devices, from_everyone(): lax.all_to_all(jnp.broadcast_to(array[None], (devices, *array.shape)), ax...  37.2 us
    all_gather x1, waiting for transfers between devices, over_pieces(): pieces = lax.all_gather(array, axis)  33.4 us
    all_to_all x5, waiting for transfers between devices, from_everyone(): lax.all_to_all(jnp.broadcast_to(array[None], (devices, *array.shape)), ax...  30.2 us
    all_gather x1, blocking collectives, broadcast(): lax.all_gather(array, axis)  24.5 us
    all_to_all x2, starting transfers between devices, sum_at_owner(): lax.all_to_all(split_up(array, dim, devices), axis, 0, 0, tiled=True)  24.1 us
    all_to_all x2, starting transfers between devices, stacked_from(): lax.all_to_all(jnp.stack([pieces] * lax.axis_size(axes[k])), axes[k], 0, 0)  19.7 us
    all_to_all x2, waiting for transfers between devices, sum_at_owner(): lax.all_to_all(split_up(array, dim, devices), axis, 0, 0, tiled=True)  14.5 us
  transfers between devices with their start and end apart: 10, of which 8 were waited for; matrix products, arithmetic and copies ran while one was open for 15% of the time, Pallas kernels for 0%

profile of v1, /device:TPU:1, one launch (start us, length us, event | category | flops | bytes accessed | tf_op | source)
XLA Modules:
  0.0 342.3 jit_solution(14451862164452213203)
XLA Ops:
  8.7 15.7 %all-to-all-start = ((bf16[16,1,7,384]{3,2,1,0:T(8,128)(2,1)}), bf16[16,1,7,384]{3,2,1,0:T(8,128)(2,1)S(1)}, u32[]{:S(2)}, u32[]{:S(2)}) async-start(bf16[16,1,7,384]{3,2,1,0:T(8,128)(2,1)} %stack.9), calls=%async_computation | async-start | bytes 196608 | tf_op jit(solution)/shard_map/all_to_all | solution.py:29
  24.4 2.3 convert_reduce_fusion
  26.8 3.0 fusion.12
  29.8 6.5 %all-to-all-done = bf16[16,1,7,384]{3,2,1,0:T(8,128)(2,1)S(1)} async-done(((bf16[16,1,7,384]{3,2,1,0:T(8,128)(2,1)}), bf16[16,1,7,384]{3,2,1,0:T(8,128)(2,1)S(1)}, u32[]{:S(2)}, u32[]{:S(2)}) %all-to-all-start) | async-done | bytes 86048 | tf_op jit(solution)/shard_map/all_to_all | solution.py:29
  37.1 4.0 %all-to-all-start.1 = ((bf16[4,16,7,384]{3,1,2,0:T(8,128)(2,1)}), bf16[4,16,7,384]{3,1,2,0:T(8,128)(2,1)S(1)}, u32[]{:S(2)}, u32[]{:S(2)}) async-start(bf16[4,16,7,384]{3,1,2,0:T(8,128)(2,1)} %stack.10), calls=%async_computation.1 | async-start | bytes 688128 | tf_op jit(solution)/shard_map/all_to_all | solution.py:29
  41.1 3.3 fusion.23
  44.4 1.5 copy.94
  47.2 8.1 %all_to_all.50 = bf16[2,64,7,384]{3,1,2,0:T(8,128)(2,1)S(1)} all-to-all(bf16[2,64,7,384]{3,1,2,0:T(8,128)(2,1)S(1)} %pad_maximum_fusion), channel_id=1, replica_groups=mesh['sample'=4,'row_0'=4,'row_1'=2,'col'=16] {'row_1'}, dimensions={0} | all-to-all | bytes 1376256 | tf_op jit(solution)/shard_map/all_to_all | solution.py:29
  61.0 3.5 %all-to-all-start.3 = ((f32[16,32,112]{2,1,0:T(8,128)}), f32[16,32,112]{2,1,0:T(8,128)S(1)}, u32[]{:S(2)}, u32[]{:S(2)}) async-start(f32[16,32,112]{2,1,0:T(8,128)} %broadcast_in_dim.28), calls=%async_computation.3 | async-start | bytes 524288 | tf_op jit(solution)/shard_map/all_to_all | solution.py:43
  65.8 12.8 %all-to-all-done.3 = f32[16,32,112]{2,1,0:T(8,128)S(1)} async-done(((f32[16,32,112]{2,1,0:T(8,128)}), f32[16,32,112]{2,1,0:T(8,128)S(1)}, u32[]{:S(2)}, u32[]{:S(2)}) %all-to-all-start.3) | async-done | bytes 229408 | tf_op jit(solution)/shard_map/all_to_all | solution.py:43
  80.5 10.2 %all-to-all-start.4 = ((bf16[16,7,384]{2,1,0:T(8,128)(2,1)}), bf16[16,7,384]{2,1,0:T(8,128)(2,1)S(1)}, u32[]{:S(2)}, u32[]{:S(2)}) async-start(bf16[16,7,384]{2,1,0:T(8,128)(2,1)} %broadcast_in_dim.29), calls=%async_computation.4 | async-start | bytes 196608 | tf_op jit(solution)/shard_map/all_to_all | solution.py:43
  90.7 11.9 %all-to-all-done.4 = bf16[16,7,384]{2,1,0:T(8,128)(2,1)S(1)} async-done(((bf16[16,7,384]{2,1,0:T(8,128)(2,1)}), bf16[16,7,384]{2,1,0:T(8,128)(2,1)S(1)}, u32[]{:S(2)}, u32[]{:S(2)}) %all-to-all-start.4) | async-done | bytes 86048 | tf_op jit(solution)/shard_map/all_to_all | solution.py:43
  105.1 6.2 %all-to-all-start.7 = ((bf16[8,56,384]{2,1,0:T(8,128)(2,1)}), bf16[8,56,384]{2,1,0:T(8,128)(2,1)S(1)}, u32[]{:S(2)}, u32[]{:S(2)}) async-start(bf16[8,56,384]{2,1,0:T(8,128)(2,1)} %broadcast_in_dim.32), calls=%async_computation.7 | async-start | bytes 688128 | tf_op jit(solution)/shard_map/all_to_all | solution.py:43
  111.3 33.4 %all-gather.3.cloned.1.call-done = f32[16,112,384]{2,1,0:T(8,128)} async-done(((f32[1,112,384]{2,1,0:T(8,128)}), f32[16,112,384]{2,1,0:T(8,128)}) %all-gather.3.cloned.1.call-update) | async-done | bytes 2752528 | tf_op jit(solution)/shard_map/all_gather | solution.py:84
  144.7 1.9 reduce_sum.111
  149.2 12.7 %all-to-all-start.6 = ((bf16[8,56,384]{2,1,0:T(8,128)(2,1)}), bf16[8,56,384]{2,1,0:T(8,128)(2,1)S(1)}, u32[]{:S(2)}, u32[]{:S(2)}) async-start(bf16[8,56,384]{2,1,0:T(8,128)(2,1)} %broadcast_in_dim.31), calls=%async_computation.6 | async-start | bytes 688128 | tf_op jit(solution)/shard_map/all_to_all | solution.py:43
  163.6 5.5 %all-to-all-done.6 = bf16[8,56,384]{2,1,0:T(8,128)(2,1)S(1)} async-done(((bf16[8,56,384]{2,1,0:T(8,128)(2,1)}), bf16[8,56,384]{2,1,0:T(8,128)(2,1)S(1)}, u32[]{:S(2)}, u32[]{:S(2)}) %all-to-all-start.6) | async-done | bytes 344096 | tf_op jit(solution)/shard_map/all_to_all | solution.py:43
  171.0 7.2 %all-to-all-start.9 = ((bf16[16,3,768]{2,1,0:T(4,128)(2,1)}), bf16[16,3,768]{2,1,0:T(4,128)(2,1)S(1)}, u32[]{:S(2)}, u32[]{:S(2)}) async-start(bf16[16,3,768]{2,1,0:T(4,128)(2,1)} %reshape.139), calls=%async_computation.9 | async-start | bytes 196608 | tf_op jit(solution)/shard_map/all_to_all | solution.py:108
  179.5 10.6 %all-to-all-done.9 = bf16[16,3,768]{2,1,0:T(4,128)(2,1)S(1)} async-done(((bf16[16,3,768]{2,1,0:T(4,128)(2,1)}), bf16[16,3,768]{2,1,0:T(4,128)(2,1)S(1)}, u32[]{:S(2)}, u32[]{:S(2)}) %all-to-all-start.9) | async-done | bytes 73760 | tf_op jit(solution)/shard_map/all_to_all | solution.py:108
  191.3 4.6 %all-to-all-start.5 = ((bf16[16,112,384]{2,1,0:T(8,128)(2,1)}), bf16[16,112,384]{2,1,0:T(8,128)(2,1)S(1)}, u32[]{:S(2)}, u32[]{:S(2)}) async-start(bf16[16,112,384]{2,1,0:T(8,128)(2,1)} %broadcast_in_dim.30), calls=%async_computation.5 | async-start | bytes 2752512 | tf_op jit(solution)/shard_map/all_to_all | solution.py:43
  195.9 1.6 copy.103
  197.6 1.6 reshape.135
  200.5 1.6 convert_element_type.148
  206.3 3.8 %convolution_bitcast_fusion = f32[128,16]{0,1:T(8,128)S(1)} fusion(bf16[16,112,56]{2,0,1:T(8,128)(2,1)} %copy.99, bf16[112,56,128]{2,1,0:T(8,128)(2,1)S(1)} %copy-done.1, f32[128]{0:T(128)S(1)} %copy-done.27, f32[112,56]{1,0:T(8,128)} %copy-done.22, f32[112,56]{1,0:T(8,128)} %copy-done.17), kind=kOutput, calls=%fused_computation.41 | convolution fusion | flops 29704192 | bytes 1865216 | tf_op jit(solution)/shard_map/ijc,hij->ch/dot_general | solution.py:197
  210.1 6.4 %fusion.11 = (f32[128]{0:T(128)S(1)}, f32[112,56]{1,0:T(8,128)S(1)}, f32[112,56]{1,0:T(8,128)}, f32[112,56,128]{2,1,0:T(8,128)}) fusion(bf16[112,56,128]{2,1,0:T(8,128)(2,1)S(1)} %copy-done.1, f32[112,56]{1,0:T(8,128)S(1)} %copy-done.23, f32[112,56]{1,0:T(8,128)S(1)} %copy-done.18, f32[128]{0:T(128)} %param.11, bf16[16,112,56]{2,0,1:T(8,128)(2,1)S(1)} %copy-done.19, ...), kind=kOutput, calls=%fused_computation.13 | convolution fusion | flops 32902784 | bytes 5123072 | tf_op jit(solution)/shard_map/hij,ch->ijc/dot_general | solution.py:196
  216.5 8.1 %all-reduce.1 = (f32[128,16]{0,1:T(8,128)S(1)}, f32[128]{0:T(128)}) all-reduce(f32[128,16]{0,1:T(8,128)S(1)} %convolution_bitcast_fusion, f32[128]{0:T(128)S(1)} %get-tuple-element.8), channel_id=1, replica_groups=mesh['sample'=4,'row_0'=4,'row_1'=2,'col'=16] {'row_0'}, use_global_device_ids=true, to_apply=%region_12.13 | all-reduce | flops 2176 | bytes 17408 | tf_op jit(solution)/shard_map/psum | solution.py:89
  224.7 5.9 %all-reduce.2 = (f32[128,16]{0,1:T(8,128)S(1)}, f32[128]{0:T(128)S(1)}) all-reduce(f32[128,16]{0,1:T(8,128)S(1)} %get-tuple-element.13, f32[128]{0:T(128)} %get-tuple-element.14), channel_id=1, replica_groups=mesh['sample'=4,'row_0'=4,'row_1'=2,'col'=16] {'row_1'}, use_global_device_ids=true, to_apply=%region_13.14 | all-reduce | flops 2176 | bytes 17408 | tf_op jit(solution)/shard_map/psum | solution.py:89
  230.5 46.1 %all-reduce = (f32[128,16]{0,1:T(8,128)}, f32[128]{0:T(128)}) all-reduce(f32[128,16]{0,1:T(8,128)S(1)} %get-tuple-element.15, f32[128]{0:T(128)S(1)} %get-tuple-element.16), channel_id=1, replica_groups=mesh['sample'=4,'row_0'=4,'row_1'=2,'col'=16] {'col'}, use_global_device_ids=true, to_apply=%region_14.15 | all-reduce | flops 2176 | bytes 17408 | tf_op jit(solution)/shard_map/psum | solution.py:89
  278.3 7.7 %fusion.10 = bf16[112,56,128]{2,1,0:T(8,128)(2,1)} fusion(bf16[112,56,128]{2,1,0:T(8,128)(2,1)S(1)} %copy-done.1, f32[112,56,128]{2,1,0:T(8,128)} %get-tuple-element.31, f32[112,56]{1,0:T(8,128)S(1)} %get-tuple-element.32, f32[112,56]{1,0:T(8,128)S(1)} %get-tuple-element.33, f32[128]{0:T(128)} %param.11, f32[112,56]{1,0:T(8,128)S(1)} %copy-done.23, ...), kind=kLoop, calls=%fused_computation.12 | loop fusion | flops 7225344 | bytes 6523392 | tf_op jit(solution)/shard_map/convert_element_type | solution.py:211
  286.9 24.5 %all-gather = bf16[896,384]{1,0:T(8,128)(2,1)S(1)} all-gather(bf16[56,384]{1,0:T(8,128)(2,1)S(1)} %fusion.19), channel_id=2, replica_groups=mesh['sample'=4,'row_0'=4,'row_1'=2,'col'=16] {'col'}, dimensions={0}, use_global_device_ids=true | all-gather | bytes 731136 | tf_op jit(solution)/shard_map/all_gather | solution.py:98
  313.1 16.9 %all-to-all-start.8 = ((bf16[8,3,768]{2,1,0:T(4,128)(2,1)}), bf16[8,3,768]{2,1,0:T(4,128)(2,1)S(1)}, u32[]{:S(2)}, u32[]{:S(2)}) async-start(bf16[8,3,768]{2,1,0:T(4,128)(2,1)} %reshape.138), calls=%async_computation.8 | async-start | bytes 98304 | tf_op jit(solution)/shard_map/all_to_all | solution.py:108
  331.0 3.8 %all-to-all-done.8 = bf16[8,3,768]{2,1,0:T(4,128)(2,1)S(1)} async-done(((bf16[8,3,768]{2,1,0:T(4,128)(2,1)}), bf16[8,3,768]{2,1,0:T(4,128)(2,1)S(1)}, u32[]{:S(2)}, u32[]{:S(2)}) %all-to-all-start.8) | async-done | bytes 36896 | tf_op jit(solution)/shard_map/all_to_all | solution.py:108
  (136 shorter events, 34.5 us)
Async XLA Ops:
  7.2 52.3 %copy-start = (bf16[384,384]{1,0:T(8,128)(2,1)S(1)}, bf16[384,384]{1,0:T(8,128)(2,1)}, u32[]{:S(2)}) copy-start(bf16[384,384]{1,0:T(8,128)(2,1)} %param.14) | copy-start | bytes 884740
  7.2 33.9 %copy-start.1 = (bf16[112,56,128]{2,1,0:T(8,128)(2,1)S(1)}, bf16[112,56,128]{2,1,0:T(8,128)(2,1)}, u32[]{:S(2)}) copy-start(bf16[112,56,128]{2,1,0:T(8,128)(2,1)} %param.10) | copy-start | bytes 4816900
  7.2 33.9 %copy-start.27 = (f32[128]{0:T(128)S(1)}, f32[128]{0:T(128)}, u32[]{:S(2)}) copy-start(f32[128]{0:T(128)} %param.11) | copy-start | bytes 1540
  7.2 33.9 %copy-start.28 = (bf16[128,16]{0,1:T(8,128)(2,1)S(1)}, bf16[128,16]{0,1:T(8,128)(2,1)}, u32[]{:S(2)}) copy-start(bf16[128,16]{0,1:T(8,128)(2,1)} %param.12) | copy-start | bytes 12292
  8.7 27.6 %all-to-all-start = ((bf16[16,1,7,384]{3,2,1,0:T(8,128)(2,1)}), bf16[16,1,7,384]{3,2,1,0:T(8,128)(2,1)S(1)}, u32[]{:S(2)}, u32[]{:S(2)}) async-start(bf16[16,1,7,384]{3,2,1,0:T(8,128)(2,1)} %stack.9), calls=%async_computation | async-start | bytes 196608 | tf_op jit(solution)/shard_map/all_to_all | solution.py:29
  26.8 17.6 %copy-start.17 = (f32[112,56]{1,0:T(8,128)}, f32[112,56]{1,0:T(8,128)S(1)}, u32[]{:S(2)}) copy-start(f32[112,56]{1,0:T(8,128)S(1)} %broadcast_multiply_fusion.2) | copy-start | bytes 75268
  29.8 16.1 %copy-start.22 = (f32[112,56]{1,0:T(8,128)}, f32[112,56]{1,0:T(8,128)S(1)}, u32[]{:S(2)}) copy-start(f32[112,56]{1,0:T(8,128)S(1)} %add_rsqrt_fusion) | copy-start | bytes 75268
  36.3 9.6 %copy-start.29 = (s32[56]{0:T(128)S(1)}, s32[56]{0:T(128)}, u32[]{:S(2)}) copy-start(s32[56]{0:T(128)} %param.18) | copy-start | bytes 676
  37.1 10.0 %all-to-all-start.1 = ((bf16[4,16,7,384]{3,1,2,0:T(8,128)(2,1)}), bf16[4,16,7,384]{3,1,2,0:T(8,128)(2,1)S(1)}, u32[]{:S(2)}, u32[]{:S(2)}) async-start(bf16[4,16,7,384]{3,1,2,0:T(8,128)(2,1)} %stack.10), calls=%async_computation.1 | async-start | bytes 688128 | tf_op jit(solution)/shard_map/all_to_all | solution.py:29
  45.9 10.8 %copy-start.3 = (bf16[384,384]{1,0:T(8,128)(2,1)S(1)}, bf16[384,384]{1,0:T(8,128)(2,1)}, u32[]{:S(2)}) copy-start(bf16[384,384]{1,0:T(8,128)(2,1)} %param.15) | copy-start | bytes 884740
  56.7 7.9 %copy-start.5 = (bf16[384,384]{1,0:T(8,128)(2,1)S(1)}, bf16[384,384]{1,0:T(8,128)(2,1)}, u32[]{:S(2)}) copy-start(bf16[384,384]{1,0:T(8,128)(2,1)} %param.16) | copy-start | bytes 884740
  57.9 21.1 %copy-start.7 = (bf16[56,384]{0,1:T(8,128)(2,1)}, bf16[56,384]{0,1:T(8,128)(2,1)S(1)}, u32[]{:S(2)}) copy-start(bf16[56,384]{0,1:T(8,128)(2,1)S(1)} %copy.93) | copy-start | bytes 129028
  59.8 20.0 %copy-start.8 = (bf16[112,384]{0,1:T(8,128)(2,1)}, bf16[112,384]{0,1:T(8,128)(2,1)S(1)}, u32[]{:S(2)}) copy-start(bf16[112,384]{0,1:T(8,128)(2,1)S(1)} %copy.92) | copy-start | bytes 258052
  59.8 20.0 %copy-start.26 = (bf16[7,384]{1,0:T(8,128)(2,1)S(1)}, bf16[7,384]{1,0:T(8,128)(2,1)}, u32[]{:S(2)}) copy-start(bf16[7,384]{1,0:T(8,128)(2,1)} %param.19) | copy-start | bytes 16132
  61.0 17.5 %all-to-all-start.3 = ((f32[16,32,112]{2,1,0:T(8,128)}), f32[16,32,112]{2,1,0:T(8,128)S(1)}, u32[]{:S(2)}, u32[]{:S(2)}) async-start(f32[16,32,112]{2,1,0:T(8,128)} %broadcast_in_dim.28), calls=%async_computation.3 | async-start | bytes 524288 | tf_op jit(solution)/shard_map/all_to_all | solution.py:43
  64.6 80.1 %all-gather.3.cloned.1.call-start = ((), (), s32[]{:S(2)}) async-start(), calls=%async_computation.10 | async-start | bytes 2924544 | tf_op jit(solution)/shard_map/all_gather | solution.py:84
  65.7 38.5 %copy-start.24 = (bf16[56,384]{0,1:T(8,128)(2,1)}, bf16[56,384]{0,1:T(8,128)(2,1)S(1)}, u32[]{:S(2)}) copy-start(bf16[56,384]{0,1:T(8,128)(2,1)S(1)} %copy.96) | copy-start | bytes 129028
  80.5 22.1 %all-to-all-start.4 = ((bf16[16,7,384]{2,1,0:T(8,128)(2,1)}), bf16[16,7,384]{2,1,0:T(8,128)(2,1)S(1)}, u32[]{:S(2)}, u32[]{:S(2)}) async-start(bf16[16,7,384]{2,1,0:T(8,128)(2,1)} %broadcast_in_dim.29), calls=%async_computation.4 | async-start | bytes 196608 | tf_op jit(solution)/shard_map/all_to_all | solution.py:43
  102.6 8.8 %copy-start.11 = (bf16[112,384]{1,0:T(8,128)(2,1)}, bf16[112,384]{1,0:T(8,128)(2,1)S(1)}, u32[]{:S(2)}) copy-start(bf16[112,384]{1,0:T(8,128)(2,1)S(1)} %reshape.131) | copy-start | bytes 258052
  105.1 42.9 %copy-start.9 = (bf16[112,384]{0,1:T(8,128)(2,1)S(1)}, bf16[112,384]{0,1:T(8,128)(2,1)}, u32[]{:S(2)}) copy-start(bf16[112,384]{0,1:T(8,128)(2,1)} %copy-done.8) | copy-start | bytes 258052
  105.1 43.3 %all-to-all-start.7 = ((bf16[8,56,384]{2,1,0:T(8,128)(2,1)}), bf16[8,56,384]{2,1,0:T(8,128)(2,1)S(1)}, u32[]{:S(2)}, u32[]{:S(2)}) async-start(bf16[8,56,384]{2,1,0:T(8,128)(2,1)} %broadcast_in_dim.32), calls=%async_computation.7 | async-start | bytes 688128 | tf_op jit(solution)/shard_map/all_to_all | solution.py:43
  146.6 44.7 %copy-start.2 = (f32[112,384]{1,0:T(8,128)}, f32[112,384]{1,0:T(8,128)S(1)}, u32[]{:S(2)}) copy-start(f32[112,384]{1,0:T(8,128)S(1)} %reduce_sum.111) | copy-start | bytes 516100
  149.2 20.0 %all-to-all-start.6 = ((bf16[8,56,384]{2,1,0:T(8,128)(2,1)}), bf16[8,56,384]{2,1,0:T(8,128)(2,1)S(1)}, u32[]{:S(2)}, u32[]{:S(2)}) async-start(bf16[8,56,384]{2,1,0:T(8,128)(2,1)} %broadcast_in_dim.31), calls=%async_computation.6 | async-start | bytes 688128 | tf_op jit(solution)/shard_map/all_to_all | solution.py:43
  169.2 22.1 %copy-start.13 = (f32[56,384]{1,0:T(8,128)}, f32[56,384]{1,0:T(8,128)S(1)}, u32[]{:S(2)}) copy-start(f32[56,384]{1,0:T(8,128)S(1)} %convert_reduce_fusion.3) | copy-start | bytes 258052
  171.0 19.1 %all-to-all-start.9 = ((bf16[16,3,768]{2,1,0:T(4,128)(2,1)}), bf16[16,3,768]{2,1,0:T(4,128)(2,1)S(1)}, u32[]{:S(2)}, u32[]{:S(2)}) async-start(bf16[16,3,768]{2,1,0:T(4,128)(2,1)} %reshape.139), calls=%async_computation.9 | async-start | bytes 196608 | tf_op jit(solution)/shard_map/all_to_all | solution.py:108
  191.3 120.8 %all-to-all-start.5 = ((bf16[16,112,384]{2,1,0:T(8,128)(2,1)}), bf16[16,112,384]{2,1,0:T(8,128)(2,1)S(1)}, u32[]{:S(2)}, u32[]{:S(2)}) async-start(bf16[16,112,384]{2,1,0:T(8,128)(2,1)} %broadcast_in_dim.30), calls=%async_computation.5 | async-start | bytes 2752512 | tf_op jit(solution)/shard_map/all_to_all | solution.py:43
  210.1 66.5 %copy-start.12 = (bf16[112,384]{1,0:T(8,128)(2,1)S(1)}, bf16[112,384]{1,0:T(8,128)(2,1)}, u32[]{:S(2)}) copy-start(bf16[112,384]{1,0:T(8,128)(2,1)} %copy-done.11) | copy-start | bytes 258052
  278.3 8.1 %copy-start.6 = (bf16[384,384]{1,0:T(8,128)(2,1)S(1)}, bf16[384,384]{1,0:T(8,128)(2,1)}, u32[]{:S(2)}) copy-start(bf16[384,384]{1,0:T(8,128)(2,1)} %param.16) | copy-start | bytes 884740
  278.3 8.1 %copy-start.16 = (f32[56,384]{1,0:T(8,128)S(1)}, f32[56,384]{1,0:T(8,128)}, u32[]{:S(2)}) copy-start(f32[56,384]{1,0:T(8,128)} %copy-done.15) | copy-start | bytes 258052
  278.3 33.1 %copy-start.21 = (bf16[16,3,768]{2,1,0:T(4,128)(2,1)S(1)}, bf16[16,3,768]{2,1,0:T(4,128)(2,1)}, u32[]{:S(2)}) copy-start(bf16[16,3,768]{2,1,0:T(4,128)(2,1)} %copy-done.20) | copy-start | bytes 221188
  286.0 26.3 %copy-start.25 = (bf16[112,24]{0,1:T(8,128)(2,1)S(1)}, bf16[112,24]{0,1:T(8,128)(2,1)}, u32[]{:S(2)}) copy-start(bf16[112,24]{0,1:T(8,128)(2,1)} %reshape.136) | copy-start | bytes 16132
  313.1 21.7 %all-to-all-start.8 = ((bf16[8,3,768]{2,1,0:T(4,128)(2,1)}), bf16[8,3,768]{2,1,0:T(4,128)(2,1)S(1)}, u32[]{:S(2)}, u32[]{:S(2)}) async-start(bf16[8,3,768]{2,1,0:T(4,128)(2,1)} %reshape.138), calls=%async_computation.8 | async-start | bytes 98304 | tf_op jit(solution)/shard_map/all_to_all | solution.py:108
  (8 other events, 33.8 us)
Sparse Core Ops, SparseCore 0:
  79.9 64.7 all-gather.2
